TPU v7x, 32 devices: a whole 2x2x4 slice. The times are simulated.
32 devices in a mesh: dp: 2 (over core), zero: 16 (over z, y, x).
Axes of the slice: x: 2, y: 2, z: 4, core: 2. Of those that a mesh axis runs over, the one named last changes fastest.
Arguments:
- tokens: bfloat16 [32768, 768], P(('dp', 'zero')), may hold values from -6 to 6
- out_grad: bfloat16 [32768, 768], P(('dp', 'zero')), may hold values from -6 to 6
- mask_pos: int32 [256, 32], P(('dp', 'zero')), may hold values from -1 to 127, as said below
- repl_id: int32 [256, 32], P(('dp', 'zero')), may hold values from 0 to 4095
- replace_embed: bfloat16 [4096, 768], replicated, may hold values from -6 to 6
- masters: float32 [16, 768, 768], P(None, 'zero'), as said below
- norm_params: float32 [4, 768], P(None, 'zero'), as said below
- first_moment: float32 [16, 768, 768], P(None, 'zero')
- second_moment: float32 [16, 768, 768], P(None, 'zero'), as said below
- left_basis: float32 [16, 768, 768], P(None, 'zero'), as said below
- right_basis: float32 [16, 768, 768], P(None, 'zero'), as said below
- norm_first: float32 [4, 768], P(None, 'zero')
- norm_second: float32 [4, 768], P(None, 'zero'), as said below
- step: int32 [1], replicated, may hold values from 1 to 20
Outputs:
- layer_out: bfloat16 [32768, 768], P(('dp', 'zero'))
- in_grad: float32 [32768, 768], P(('dp', 'zero'))
- new_first: float32 [16, 768, 768], P(None, 'zero')
- new_second: float32 [16, 768, 768], P(None, 'zero')
- new_master: float32 [16, 768, 768], P(None, 'zero')
- new_copy: bfloat16 [16, 768, 768], P(None, 'zero')
- new_norm_first: float32 [4, 768], P(None, 'zero')
- new_norm_second: float32 [4, 768], P(None, 'zero')
- new_norms: float32 [4, 768], P(None, 'zero')
Inputs may be any that keep to these rules, and one draw needn't show every extreme that they name: `mask_pos`: in each sequence the entries other than -1 are distinct positions and stand in the first slots; a sequence has 1 to 32 of them. `masters`: tiles 0 to 2, the gate and up tiles, tile 3 and the down tiles have entries of deviation about 768^-0.5, (4/768)^0.5, and (2/3072)^0.5. `norm_params`: rows 0 and 2 are gains within 0.7 to 1.3; rows 1 and 3 are shifts. `second_moment`: every entry is positive. `left_basis`: each tile's basis is orthogonal. `right_basis`: each tile's basis is orthogonal. `norm_second`: every entry is positive.
All inputs are finite; a program needn't handle non-finite values.
Results may differ from a plain program's by a relative error of at most 0.0075.
The roundings to bfloat16 on the way count: a program that leaves them out, or rounds other values in their place, can miss the bound.
Values may be sent and summed in bfloat16 or wider, within the bound.
A program may use at most 256 MiB of HBM per device.

v0:
```python
import math
import jax
import jax.numpy as jnp
import numpy as np
from jax import lax
from jax.sharding import PartitionSpec as P

HEADS = 12
CAP = 1
highest = lax.Precision.HIGHEST
norm_eps = 1e-12
beta_one = 0.9
beta_two = 0.95
adam_eps = 1e-08
peak_rate = 0.1
warm_steps = 5.0
total_steps = 60.0
decay_rate = 0.01


def alibi_slopes(head_count):

    def power_slopes(power_count):
        first_slope = 2.0 ** (-8.0 / power_count)
        return [first_slope ** (position + 1) for position in range(power_count)]

    nearest = 2 ** int(math.floor(math.log2(head_count)))
    slope_list = power_slopes(nearest)
    slope_list = slope_list + power_slopes(2 * nearest)[0::2][: head_count - nearest]
    return np.array(slope_list, np.float32)


def layer_norm(values, gain_row, shift_row):
    row_mean = jnp.mean(values, axis=-1, keepdims=True)
    centered = values - row_mean
    spread = jnp.mean(centered * centered, axis=-1, keepdims=True)
    return centered * lax.rsqrt(spread + norm_eps) * gain_row + shift_row


def gated(gate_val, up_value):
    return jax.nn.gelu(gate_val, approximate=False) * up_value


def shards(
    tokens,
    out_grad,
    mask_pos,
    repl_id,
    replace_embed,
    masters,
    norm_params,
    first_moment,
    second_moment,
    left_basis,
    right_basis,
    norm_first,
    norm_second,
    step,
):
    seq_count = mask_pos.shape[0]
    tok_rows, model_width = tokens.shape
    length = tok_rows // seq_count
    head_count = HEADS
    head_size = model_width // head_count
    score_scale = float(head_size) ** (-0.5)
    tile_count = masters.shape[0]
    ff_parts = (tile_count - 4) // 3
    shard_rows = masters.shape[1]
    positions = jnp.arange(length, dtype=jnp.int32)
    mask_hits = mask_pos[:, :, None] == positions[None, None, :]
    masked = jnp.any(mask_hits, axis=1).reshape(-1, 1)
    row_ids = jnp.sum(jnp.where(mask_hits, repl_id[:, :, None], 0), axis=1).reshape(-1)
    inputs = jnp.where(masked, jnp.take(replace_embed, row_ids, axis=0), tokens)
    shard_low = masters.astype(jnp.bfloat16)
    whole_tiles, norm_whole = (
        lax.all_gather(shard_low, "zero", axis=1, tiled=True),
        lax.all_gather(norm_params.astype(jnp.bfloat16), "zero", axis=1, tiled=True),
    )
    norm_gains = norm_whole.astype(jnp.float32)
    slopes = jnp.asarray(alibi_slopes(head_count))
    distance = jnp.abs(positions[:, None] - positions[None, :]).astype(jnp.float32)
    alibi_bias = -slopes[:, None, None] * distance[None]
    head_shape = (seq_count, length, head_count, head_size)
    qkv_low = jnp.einsum(
        "td,kde->kte", inputs, whole_tiles[0:3], preferred_element_type=jnp.float32
    ).astype(jnp.bfloat16)
    queries = qkv_low[0].reshape(head_shape)
    key_rows = qkv_low[1].reshape(head_shape)
    values = qkv_low[2].reshape(head_shape)

    def score_block():
        raw_scores = jnp.einsum(
            "bqhd,bkhd->bhqk", queries, key_rows, preferred_element_type=jnp.float32
        )
        return raw_scores * score_scale + alibi_bias[None]

    scores = score_block()
    row_max = jnp.max(scores, axis=-1, keepdims=True)
    log_total = row_max + jnp.log(jnp.sum(jnp.exp(scores - row_max), axis=-1, keepdims=True))
    soft_low = jnp.exp(scores - log_total).astype(jnp.bfloat16)
    mixed_low = jnp.einsum("bhqk,bkhd->bqhd", soft_low, values, preferred_element_type=jnp.float32)
    mixed_low = mixed_low.reshape(tok_rows, model_width).astype(jnp.bfloat16)
    attended = jnp.dot(mixed_low, whole_tiles[3], preferred_element_type=jnp.float32)
    first_sum = inputs.astype(jnp.float32) + attended
    hidden, first_back = jax.vjp(layer_norm, first_sum, norm_gains[0], norm_gains[1])
    hidden_low = hidden.astype(jnp.bfloat16)
    gate_up = jnp.einsum(
        "td,fde->tfe",
        hidden_low,
        whole_tiles[4 : 4 + 2 * ff_parts],
        preferred_element_type=jnp.float32,
    )
    gate_val = gate_up[:, :ff_parts].reshape(tok_rows, ff_parts * model_width)
    up_value = gate_up[:, ff_parts:].reshape(tok_rows, ff_parts * model_width)
    inner_act, inner_back = jax.vjp(gated, gate_val, up_value)
    inner_low = inner_act.astype(jnp.bfloat16).reshape(tok_rows, ff_parts, model_width)
    branch = jnp.einsum(
        "tfe,fed->td",
        inner_low,
        whole_tiles[4 + 2 * ff_parts :],
        preferred_element_type=jnp.float32,
    )
    layer_out, second_back = jax.vjp(layer_norm, hidden + branch, norm_gains[2], norm_gains[3])
    back_tiles = lax.all_gather(shard_low, "zero", axis=1, tiled=True)
    d_second, d_gain_two, d_shift_two = second_back(out_grad.astype(jnp.float32))
    d_branch = d_second.astype(jnp.bfloat16)
    grad_down = jnp.einsum("tfe,td->fed", inner_low, d_branch, preferred_element_type=jnp.float32)
    d_inner = jnp.einsum(
        "td,fed->tfe", d_branch, back_tiles[4 + 2 * ff_parts :], preferred_element_type=jnp.float32
    )
    d_gate, d_up = inner_back(d_inner.reshape(tok_rows, ff_parts * model_width))
    d_gate_up = jnp.concatenate(
        [
            d_gate.reshape(tok_rows, ff_parts, model_width),
            d_up.reshape(tok_rows, ff_parts, model_width),
        ],
        axis=1,
    ).astype(jnp.bfloat16)
    grad_gate_up = jnp.einsum(
        "td,tfe->fde", hidden_low, d_gate_up, preferred_element_type=jnp.float32
    )
    d_hidden = d_second + jnp.einsum(
        "tfe,fde->td",
        d_gate_up,
        back_tiles[4 : 4 + 2 * ff_parts],
        preferred_element_type=jnp.float32,
    )
    d_first, d_gain_one, d_shift_one = first_back(d_hidden)
    d_attended = d_first.astype(jnp.bfloat16)
    grad_out = jnp.einsum("td,te->de", mixed_low, d_attended, preferred_element_type=jnp.float32)
    d_mixed = jnp.einsum("te,de->td", d_attended, back_tiles[3], preferred_element_type=jnp.float32)
    d_mixed = d_mixed.astype(jnp.bfloat16).reshape(head_shape)
    again_probs = jnp.exp(score_block() - log_total)
    again_low = again_probs.astype(jnp.bfloat16)
    d_probs = jnp.einsum("bqhd,bkhd->bhqk", d_mixed, values, preferred_element_type=jnp.float32)
    row_delta = jnp.sum(again_probs * d_probs, axis=-1, keepdims=True)
    d_scores = (again_probs * (d_probs - row_delta)).astype(jnp.bfloat16)
    d_query = (
        jnp.einsum("bhqk,bkhd->bqhd", d_scores, key_rows, preferred_element_type=jnp.float32)
        * score_scale
    )
    d_keys = (
        jnp.einsum("bhqk,bqhd->bkhd", d_scores, queries, preferred_element_type=jnp.float32)
        * score_scale
    )
    d_values = jnp.einsum("bhqk,bqhd->bkhd", again_low, d_mixed, preferred_element_type=jnp.float32)
    d_qkv = (
        jnp.stack([d_query, d_keys, d_values])
        .reshape(3, tok_rows, model_width)
        .astype(jnp.bfloat16)
    )
    grad_qkv = jnp.einsum("td,kte->kde", inputs, d_qkv, preferred_element_type=jnp.float32)
    d_inputs = d_first + jnp.einsum(
        "kte,kde->td", d_qkv, back_tiles[0:3], preferred_element_type=jnp.float32
    )
    in_grad = jnp.where(masked, 0.0, d_inputs)
    tile_grads = jnp.concatenate([grad_qkv, grad_out[None], grad_gate_up, grad_down], axis=0)
    norm_grads = jnp.stack([d_gain_one, d_shift_one, d_gain_two, d_shift_two])
    step_value = step[0].astype(jnp.float32)
    step_rate = peak_rate * jnp.minimum(
        step_value / warm_steps, (total_steps - step_value) / (total_steps - warm_steps)
    )
    fix_one = 1.0 - jnp.power(beta_one, step_value)
    fix_two = 1.0 - jnp.power(beta_two, step_value)
    devices = lax.axis_size("zero")
    capacity = CAP
    target = jnp.arange(tile_count, dtype=jnp.int32)
    slot_index = jnp.arange(devices * capacity, dtype=jnp.int32)
    source = jnp.where(slot_index < tile_count, slot_index, 0)

    def outgoing(source_array):
        return jnp.take(source_array, source, axis=0).reshape(
            devices, capacity, shard_rows, model_width
        )

    tile_sum, norm_sum = (
        lax.psum_scatter(tile_grads, "zero", scatter_dimension=1, tiled=True),
        lax.psum_scatter(norm_grads, "zero", scatter_dimension=1, tiled=True),
    )
    tile_sum, norm_sum = lax.psum((tile_sum, norm_sum), "dp")
    left_whole = lax.all_to_all(
        outgoing(left_basis), "zero", split_axis=0, concat_axis=2, tiled=True
    )
    right_whole = lax.all_to_all(
        outgoing(right_basis), "zero", split_axis=0, concat_axis=2, tiled=True
    )
    rotated = jnp.einsum(
        "akji,akjl->akil",
        left_whole,
        lax.all_to_all(outgoing(tile_sum), "zero", split_axis=0, concat_axis=2, tiled=True),
        precision=highest,
    )
    rotated = jnp.einsum("akil,aklm->akim", rotated, right_whole, precision=highest)
    moment_one = (
        beta_one
        * lax.all_to_all(outgoing(first_moment), "zero", split_axis=0, concat_axis=2, tiled=True)
        + (1.0 - beta_one) * rotated
    )
    moment_two = (
        beta_two
        * lax.all_to_all(outgoing(second_moment), "zero", split_axis=0, concat_axis=2, tiled=True)
        + (1.0 - beta_two) * rotated * rotated
    )
    direction = moment_one / fix_one / (jnp.sqrt(moment_two / fix_two) + adam_eps)
    update = jnp.einsum("akij,akjl->akil", left_whole, direction, precision=highest)
    update = jnp.einsum("akil,akml->akim", update, right_whole, precision=highest)
    results = jnp.stack([moment_one, moment_two, update], axis=2)
    returned = lax.all_to_all(results, "zero", split_axis=3, concat_axis=0, tiled=True)
    returned = returned.reshape(devices * capacity, 3, shard_rows, model_width)
    owned_back = jnp.take(returned, target, axis=0)
    new_master = masters - step_rate * (owned_back[:, 2] + decay_rate * masters)
    new_norm_first = beta_one * norm_first + (1.0 - beta_one) * norm_sum
    new_norm_second = beta_two * norm_second + (1.0 - beta_two) * norm_sum * norm_sum
    new_norms = norm_params - step_rate * (new_norm_first / fix_one) / (
        jnp.sqrt(new_norm_second / fix_two) + adam_eps
    )
    return (
        layer_out.astype(jnp.bfloat16),
        in_grad,
        owned_back[:, 0],
        owned_back[:, 1],
        new_master,
        new_master.astype(jnp.bfloat16),
        new_norm_first,
        new_norm_second,
        new_norms,
    )


def solution(mesh):
    in_specs = (
        P(("dp", "zero"), None),
        P(("dp", "zero"), None),
        P(("dp", "zero"), None),
        P(("dp", "zero"), None),
        P(),
        P(None, "zero", None),
        P(None, "zero"),
        P(None, "zero", None),
        P(None, "zero", None),
        P(None, "zero", None),
        P(None, "zero", None),
        P(None, "zero"),
        P(None, "zero"),
        P(),
    )
    out_specs = (
        P(("dp", "zero"), None),
        P(("dp", "zero"), None),
        P(None, "zero", None),
        P(None, "zero", None),
        P(None, "zero", None),
        P(None, "zero", None),
        P(None, "zero"),
        P(None, "zero"),
        P(None, "zero"),
    )
    return jax.shard_map(shards, mesh=mesh, in_specs=in_specs, out_specs=out_specs, check_vma=False)
```

profile of v0, /device:TPU:0, one launch (start us, length us, event | category | flops | bytes accessed | tf_op | source)
XLA Modules:
  0.0 1709.1 jit_solution(17990816463985661530)
XLA Ops:
  15.6 9.2 gather_fusion
  27.4 43.7 %all-gather = bf16[16,48,4]{1,2,0:T(4,128)(2,1)S(1)} all-gather(bf16[1,48,4]{1,2,0:T(4,128)(2,1)S(1)} %convert_bitcast_fusion.1), channel_id=1, replica_groups=mesh['dp'=2,'zero'=16] {'zero'}, dimensions={0}, use_global_device_ids=true | all-gather | bytes 6528 | tf_op jit(solution)/shard_map/all_gather | solution.py:77
  74.8 150.4 %all-gather.3.cloned.1.call-done = bf16[16,768,768]{2,1,0:T(8,128)(2,1)} async-done(((bf16[16,48,768]{2,1,0:T(8,128)(2,1)}), bf16[16,768,768]{2,1,0:T(8,128)(2,1)}) %all-gather.3.cloned.1.call-update) | async-done | bytes 18874384 | tf_op jit(solution)/shard_map/all_gather | solution.py:76
  225.2 6.4 convert_bitcast_fusion
  260.9 19.5 %fusion.9 = f32[1024,8,768]{2,0,1:T(8,128)} fusion(bf16[16,768,768]{2,1,0:T(8,128)(2,1)} %all-gather.3.cloned.1.call-done, f32[1024,768]{0,1:T(8,128)S(1)} %get-tuple-element.114, f32[768]{0:T(1024)S(1)} %get-tuple-element.83, f32[768]{0:T(1024)S(1)} %get-tuple-element.84, f32[1024]{0:T(1024)S(1)} %fusion.81, f32[1024]{0:T(1024)S(1)} %broadcast_multiply_fusion.4), kind=kOutput, calls=%fused_computation.31 | convolution fusion | flops 9667608576 | bytes 37763072 | tf_op jit(solution)/shard_map/td,fde->tfe/dot_general | solution.py:107
  280.4 29.9 %multiply_convert_fusion.1 = (bf16[1024,4,768]{2,0,1:T(8,128)(2,1)S(1)}, f32[1024,4,768]{2,0,1:T(8,128)}) fusion(f32[1024,8,768]{2,0,1:T(8,128)} %fusion.9), kind=kLoop, calls=%fused_computation.13 | loop fusion | flops 207618048 | bytes 44040192 | tf_op jit(solution)/shard_map/convert_element_type | solution.py:116
  310.4 9.3 fusion.101
  324.2 24.4 %add_convert_fusion = (bf16[1024,4,768]{2,0,1:T(8,128)(2,1)}, bf16[1024,4,768]{2,0,1:T(8,128)(2,1)}) fusion(f32[1024,4,768]{2,0,1:T(8,128)} %get-tuple-element.93, f32[1024,8,768]{2,0,1:T(8,128)} %fusion.9, bf16[16,768,768]{2,1,0:T(8,128)(2,1)} %all-gather.3.cloned.1.call-done, f32[1024]{0:T(1024)S(1)} %negate_multiply_fusion.2, ...), kind=kOutput, calls=%fused_computation.12 | convolution fusion | flops 4895539200 | bytes 59788288 | tf_op jit(solution)/shard_map/td,fed->tfe/dot_general | solution.py:128
  348.6 24.5 %multiply_reduce_fusion.1 = (f32[768]{0:T(1024)}, f32[1024]{0:T(1024)S(1)}, f32[768]{0:T(1024)}, f32[1024,768]{0,1:T(8,128)}) fusion(f32[1024,768]{0,1:T(8,128)} %copy-done.12, f32[1024]{0:T(1024)S(1)} %fusion.81, f32[1024]{0:T(1024)S(1)} %broadcast_multiply_fusion.4, f32[768]{0:T(1024)S(1)} %get-tuple-element.84, ...), kind=kOutput, calls=%fused_computation.65 | convolution fusion | flops 9683334144 | bytes 33071104 | tf_op jit(solution)/shard_map/tfe,fde->td/dot_general | solution.py:142
  373.1 3.7 fusion.97
  378.4 3.9 convolution_convert_fusion.1
  387.2 5.2 fusion.57
  392.4 4.6 multiply_reduce_fusion
  405.7 8.2 fusion.77
  413.9 18.5 %fusion.12 = f32[8,768,768]{1,2,0:T(8,128)} fusion(bf16[1024,4,768]{2,0,1:T(8,128)(2,1)} %get-tuple-element.95, bf16[1024,4,768]{2,0,1:T(8,128)(2,1)} %get-tuple-element.94, f32[1024,768]{0,1:T(8,128)} %copy-done.12, f32[768]{0:T(1024)S(1)} %get-tuple-element.83, f32[768]{0:T(1024)S(1)} %get-tuple-element.84, f32[1024]{0:T(1024)S(1)} %fusion.81, ...), kind=kOutput, calls=%fused_computation.34 | convolution fusion | flops 9673900032 | bytes 34617344 | tf_op jit(solution)/shard_map/td,tfe->fde/dot_general | solution.py:139
  432.4 5.2 convolution_bitcast_fusion.2
  440.0 3.7 stack.33
  446.3 3.8 copy.317
  450.1 3.7 stack.32
  456.3 3.8 copy.314
  460.1 3.7 stack.31
  466.6 9.7 convolution_bitcast_fusion
  476.3 26.0 %pad_maximum_fusion = f32[16,768,768]{1,2,0:T(8,128)} fusion(f32[4,768,768]{1,2,0:T(8,128)} %fusion.77, f32[8,768,768]{1,2,0:T(8,128)} %fusion.12, f32[1,768,768]{1,2,0:T(8,128)} %convolution_bitcast_fusion.2, f32[3,768,768]{1,2,0:T(8,128)} %convolution_bitcast_fusion), kind=kLoop, calls=%fused_computation.7 | loop fusion | flops 28311552 | bytes 75497472 | tf_op jit(solution)/shard_map/concatenate | solution.py:177
  502.2 37.9 %copy.333 = f32[16,768,768]{2,0,1:T(8,128)} copy(f32[16,768,768]{1,2,0:T(8,128)} %pad_maximum_fusion) | data formatting | bytes 75497472 | tf_op jit(solution)/shard_map/concatenate | solution.py:177
  540.3 538.9 %reduce-scatter.5.cloned.1.call-done = f32[16,48,768]{2,0,1:T(8,128)} async-done(((f32[16,768,768]{2,0,1:T(8,128)}), f32[16,48,768]{2,0,1:T(8,128)}) %reduce-scatter.5.cloned.1.call-update) | async-done | bytes 2359312 | tf_op jit(solution)/shard_map/reduce_scatter | solution.py:197
  1079.1 4.4 copy.334
  1085.7 3.8 gather_fusion.3
  1089.6 3.8 gather_fusion.5
  1093.4 3.8 gather_fusion.2
  1097.2 7.6 all-reduce.2.cloned.1.call-done
  1104.8 3.8 gather_fusion.4
  1108.5 7.8 select_bitcast_fusion
  1116.4 62.3 %all_to_all.60 = f32[16,1,48,768]{3,2,1,0:T(8,128)} all-to-all(f32[16,1,48,768]{3,2,1,0:T(8,128)} %get-tuple-element.107), channel_id=1, replica_groups=mesh['dp'=2,'zero'=16] {'zero'}, dimensions={0} | all-to-all | bytes 4718592 | tf_op jit(solution)/shard_map/all_to_all | solution.py:201
  1178.7 57.7 %all_to_all.61 = f32[16,1,48,768]{3,2,1,0:T(8,128)} all-to-all(f32[16,1,48,768]{3,2,1,0:T(8,128)S(1)} %get-tuple-element.106), channel_id=1, replica_groups=mesh['dp'=2,'zero'=16] {'zero'}, dimensions={0} | all-to-all | bytes 4718592 | tf_op jit(solution)/shard_map/all_to_all | solution.py:221
  1236.4 57.8 %all_to_all.62 = f32[16,1,48,768]{3,2,1,0:T(8,128)} all-to-all(f32[16,1,48,768]{3,2,1,0:T(8,128)S(1)} %get-tuple-element.110), channel_id=1, replica_groups=mesh['dp'=2,'zero'=16] {'zero'}, dimensions={0} | all-to-all | bytes 4718592 | tf_op jit(solution)/shard_map/all_to_all | solution.py:216
  1294.2 57.8 %all_to_all.63 = f32[16,1,48,768]{3,2,1,0:T(8,128)} all-to-all(f32[16,1,48,768]{3,2,1,0:T(8,128)S(1)} %get-tuple-element.108), channel_id=1, replica_groups=mesh['dp'=2,'zero'=16] {'zero'}, dimensions={0} | all-to-all | bytes 4718592 | tf_op jit(solution)/shard_map/all_to_all | solution.py:210
  1352.0 4.8 all-to-all-start.3
  1364.3 7.7 fusion.37
  1372.0 31.2 %all-to-all-done.3 = f32[16,1,48,768]{3,2,1,0:T(8,128)} async-done(((f32[16,1,48,768]{3,2,1,0:T(8,128)}), f32[16,1,48,768]{3,2,1,0:T(8,128)}, u32[]{:S(2)}, u32[]{:S(2)}) %all-to-all-start.3) | async-done | bytes 2359328 | tf_op jit(solution)/shard_map/all_to_all | solution.py:204
  1403.1 10.2 fusion.31
  1413.4 6.5 fusion.40
  1419.9 7.9 convolution_bitcast_fusion.1
  1428.3 10.4 copy.336
  1438.6 10.9 all-to-all-start.5
  1450.7 10.0 fusion.23
  1463.3 3.6 copy.340
  1466.9 209.3 %reduce-scatter.7.cloned.1.call-done = f32[48,4]{1,0:T(8,128)} async-done(((f32[768,4]{1,0:T(8,128)}), f32[48,4]{1,0:T(8,128)}) %reduce-scatter.7.cloned.1.call-update) | async-done | bytes 784
  1687.0 7.0 gather_fusion.1
  (162 shorter events, 105.8 us)
Async XLA Ops:
  7.2 1076.4 %copy-start = (f32[16,48,768]{2,1,0:T(8,128)S(1)}, f32[16,48,768]{2,1,0:T(8,128)}, u32[]{:S(2)}) copy-start(f32[16,48,768]{2,1,0:T(8,128)} %param.25) | copy-start | bytes 7077892
  7.2 218.0 %all-gather.3.cloned.1.call-start = ((), (), s32[]{:S(2)}) async-start(), calls=%async_computation.8 | async-start | bytes 20054016 | tf_op jit(solution)/shard_map/all_gather | solution.py:76
  10.2 5.2 copy-start.24
  10.2 5.2 copy-start.27
  10.2 1068.9 %reduce-scatter.5.cloned.1.call-start = ((), (), s32[]{:S(2)}) async-start(), calls=%async_computation.9 | async-start | bytes 40108032 | tf_op jit(solution)/shard_map/reduce_scatter | solution.py:197
  24.8 2.6 copy-start.25
  24.8 46.6 %copy-start.34 = (f32[12]{0:T(128)S(1)}, f32[12]{0:T(128)}, u32[]{:S(2)}) copy-start(f32[12]{0:T(128)} %constant.173) | copy-start | bytes 148
  71.3 160.2 %copy-start.30 = (pred[8,128]{1,0:T(8,128)(4,1)}, pred[8,128]{1,0:T(8,128)(4,1)S(1)}, u32[]{:S(2)}) copy-start(pred[8,128]{1,0:T(8,128)(4,1)S(1)} %fusion.80) | copy-start | bytes 3076
  248.1 2.0 copy-start.2
  250.1 1.6 copy-start.4
  251.6 2.7 copy-start.1
  251.7 2.7 copy-start.8
  255.9 1.4 copy-start.21
  257.1 3.4 copy-start.20
  260.5 49.8 %copy-start.12 = (f32[1024,768]{0,1:T(8,128)}, f32[1024,768]{0,1:T(8,128)S(1)}, u32[]{:S(2)}) copy-start(f32[1024,768]{0,1:T(8,128)S(1)} %get-tuple-element.114) | copy-start | bytes 9437188
  310.4 9.4 copy-start.15
  310.4 9.4 copy-start.6
  319.8 4.4 copy-start.10
  376.8 1.6 copy-start.16
  387.2 5.2 copy-start.9
  387.2 9.8 slice-start
  392.4 4.6 slice-start.1
  392.4 12.5 slice-start.2
  397.0 2.3 copy-start.5
  397.0 7.9 slice-start.3
  399.3 3.4 copy-start.3
  402.8 2.1 copy-start.7
  402.8 2.9 copy-start.11
  540.2 564.6 %all-reduce.2.cloned.1.call-start = ((), (), s32[]{:S(2)}) async-start(), calls=%async_computation.10 | async-start | bytes 4718592 | tf_op jit(solution)/shard_map/psum | solution.py:200
  1352.0 51.1 %all-to-all-start.3 = ((f32[16,1,48,768]{3,2,1,0:T(8,128)}), f32[16,1,48,768]{3,2,1,0:T(8,128)}, u32[]{:S(2)}, u32[]{:S(2)}) async-start(f32[16,1,48,768]{3,2,1,0:T(8,128)} %get-tuple-element.109), calls=%async_computation.4 | async-start | bytes 4718592 | tf_op jit(solution)/shard_map/all_to_all | solution.py:204
  1356.9 4.2 copy-start.13
  1361.0 2.5 copy-start.17
  1361.0 3.2 copy-start.19
  1403.1 10.2 copy-start.18
  1438.6 11.0 copy-start.23
  1438.6 11.0 copy-start.22
  1438.6 11.0 copy-start.29
  1438.6 11.1 copy-start.28
  1438.6 12.1 copy-start.31
  1438.6 241.4 %all-to-all-start.5 = ((f32[1,1,3,768,768]{4,1,2,0,3:T(1,128)}), f32[1,1,3,768,768]{4,1,2,0,3:T(1,128)}, u32[]{:S(2)}, u32[]{:S(2)}) async-start(f32[1,1,3,768,768]{4,1,2,0,3:T(1,128)} %copy.336), calls=%async_computation.6 | async-start | bytes 14155776 | tf_op jit(solution)/shard_map/all_to_all | solution.py:228
  1449.5 226.6 %reduce-scatter.7.cloned.1.call-start = ((), (), s32[]{:S(2)}) async-start(), calls=%async_computation.11 | async-start | bytes 417792
  1463.3 216.1 %copy-start.26 = (f32[4,48]{1,0:T(4,128)S(1)}, f32[4,48]{1,0:T(4,128)}, u32[]{:S(2)}) copy-start(f32[4,48]{1,0:T(4,128)} %param.23) | copy-start | bytes 2308
  1463.3 216.1 %copy-start.32 = (f32[4,48]{1,0:T(4,128)S(1)}, f32[4,48]{1,0:T(4,128)}, u32[]{:S(2)}) copy-start(f32[4,48]{1,0:T(4,128)} %param.29) | copy-start | bytes 2308
  1463.3 216.1 %copy-start.33 = (f32[4,48]{1,0:T(4,128)S(1)}, f32[4,48]{1,0:T(4,128)}, u32[]{:S(2)}) copy-start(f32[4,48]{1,0:T(4,128)} %param.28) | copy-start | bytes 2308
  1697.5 2.6 copy-start.14
Sparse Core Ops, SparseCore 0:
  11.3 213.8 all-gather.2
  540.3 538.7 reduce-scatter.4
  1083.7 21.0 all-reduce.1
  1455.2 220.8 reduce-scatter.6
where the time goes:
time: 1720 us; the launch traced here: 1710 us
  waiting for transfers between devices  937 us (54%)
  blocking collectives  282 us (16%)
  matrix products  194 us (11%)
  local copies, waits for them, and re-layouts  170 us (10%)
  other arithmetic  94.5 us (5%)
    reduce_scatter x1, waiting for transfers between devices, shards(): lax.psum_scatter(tile_grads, 'zero', scatter_dimension=1, tiled=True)  539 us
    unnamed x5, waiting for transfers between devices  209 us
    all_gather x1, waiting for transfers between devices, shards(): lax.all_gather(shard_low, 'zero', axis=1, tiled=True)  150 us
    all_to_all x1, blocking collectives, shards(): lax.all_to_all(outgoing(left_basis), 'zero', split_axis=0, concat_axis=2,...  62.3 us
    all_to_all x1, blocking collectives, shards(): lax.all_to_all(outgoing(first_moment), 'zero', split_axis=0, concat_axis=...  57.8 us
    all_to_all x1, blocking collectives, shards(): lax.all_to_all(outgoing(tile_sum), 'zero', split_axis=0, concat_axis=2, t...  57.8 us
    all_to_all x1, blocking collectives, shards(): lax.all_to_all(outgoing(second_moment), 'zero', split_axis=0, concat_axis...  57.7 us
    all_gather x1, blocking collectives, shards(): lax.all_gather(norm_params.astype(jnp.bfloat16), 'zero', axis=1, tiled=True)  43.7 us
  transfers between devices with their start and end apart: 6, of which 5 were waited for; matrix products, arithmetic and copies ran while one was open for 4% of the time, Pallas kernels for 0%

commit v1 on v0

--- a/solution.py
+++ b/solution.py
@@ -16,6 +16,31 @@
 warm_steps = 5.0
 total_steps = 60.0
 decay_rate = 0.01
+
+
+def build_ways(page, dimension_no):
+    low = list(page.shape[1:])
+    low[dimension_no] *= page.shape[0]
+    return jnp.moveaxis(page, 0, dimension_no).reshape(low)
+
+
+def columns_refer(patch, net_axis):
+    next_value = patch[None]
+    n_blocks = lax.psum(1, net_axis)
+    for q in range(n_blocks.bit_length() - 1):
+        inter = 1 << q
+        y1 = tuple(((k, k ^ inter) for k in range(n_blocks)))
+        high = lax.ppermute(next_value, net_axis, y1)
+        n_now = jnp.stack([next_value, high], axis=0)
+        top = lax.axis_index(net_axis)
+        back = top >> q & 1
+        next_value = jnp.where(back == 0, n_now, n_now[::-1]).reshape(-1, *patch.shape)
+    return next_value
+
+
+def rails_scan(unit, panel, pos_dim):
+    block_out = columns_refer(unit, panel)
+    return build_ways(block_out, pos_dim)
 
 
 def alibi_slopes(head_count):
@@ -74,7 +99,7 @@
     shard_low = masters.astype(jnp.bfloat16)
     whole_tiles, norm_whole = (
         lax.all_gather(shard_low, "zero", axis=1, tiled=True),
-        lax.all_gather(norm_params.astype(jnp.bfloat16), "zero", axis=1, tiled=True),
+        rails_scan(norm_params.astype(jnp.bfloat16), "zero", 1),
     )
     norm_gains = norm_whole.astype(jnp.float32)
     slopes = jnp.asarray(alibi_slopes(head_count))

time: 1720 us -> 1720 us (level)
  blocking collectives: 282 us -> 238 us
  waiting for transfers between devices: 937 us -> 972 us
    all_gather x1 -> x0, blocking collectives: 43.7 us -> none  [shards(): lax.all_gather(norm_params.astype(jnp.bfloat16), 'zero', axis=1, tiled=True)]
    all_gather x1, waiting for transfers between devices: 150 us -> 182 us  [shards(): lax.all_gather(shard_low, 'zero', axis=1, tiled=True)]
  transfers between devices with their start and end apart: 6 -> 10, of which waited for: 5 -> 7; matrix products, arithmetic and copies ran while one was open for 4% -> 4% of each run, Pallas kernels for 0% -> 0%
where the time goes in v1:
time: 1720 us; the launch traced here: 1710 us
  waiting for transfers between devices  972 us (57%)
  blocking collectives  238 us (14%)
  matrix products  194 us (11%)
  local copies, waits for them, and re-layouts  171 us (10%)
  other arithmetic  94.6 us (6%)
  starting transfers between devices  24.5 us (1%)
    reduce_scatter x1, waiting for transfers between devices, shards(): lax.psum_scatter(tile_grads, 'zero', scatter_dimension=1, tiled=True)  539 us
    unnamed x5, waiting for transfers between devices  209 us
    all_gather x1, waiting for transfers between devices, shards(): lax.all_gather(shard_low, 'zero', axis=1, tiled=True)  182 us
    all_to_all x1, blocking collectives, shards(): lax.all_to_all(outgoing(left_basis), 'zero', split_axis=0, concat_axis=2,...  62.3 us
    all_to_all x1, blocking collectives, shards(): lax.all_to_all(outgoing(first_moment), 'zero', split_axis=0, concat_axis=...  57.8 us
    all_to_all x1, blocking collectives, shards(): lax.all_to_all(outgoing(tile_sum), 'zero', split_axis=0, concat_axis=2, t...  57.8 us
    all_to_all x1, blocking collectives, shards(): lax.all_to_all(outgoing(second_moment), 'zero', split_axis=0, concat_axis...  57.7 us
    concatenate x1, local copies, waits for them, and re-layouts, shards(): jnp.concatenate([grad_qkv, grad_out[None], grad_gate_up, grad_down], axis=0)  37.9 us
  transfers between devices with their start and end apart: 10, of which 7 were waited for; matrix products, arithmetic and copies ran while one was open for 4% of the time, Pallas kernels for 0%

profile of v1, /device:TPU:0, one launch (start us, length us, event | category | flops | bytes accessed | tf_op | source)
XLA Modules:
  0.0 1709.3 jit_solution(2418287397995983281)
XLA Ops:
  16.1 9.2 gather_fusion
  43.0 182.2 %all-gather.2.cloned.1.call-done = bf16[16,768,768]{2,1,0:T(8,128)(2,1)} async-done(((bf16[16,48,768]{2,1,0:T(8,128)(2,1)}), bf16[16,768,768]{2,1,0:T(8,128)(2,1)}) %all-gather.2.cloned.1.call-update) | async-done | bytes 18874384 | tf_op jit(solution)/shard_map/all_gather | solution.py:101
  225.2 6.4 convert_bitcast_fusion
  261.0 19.5 %fusion.9 = f32[1024,8,768]{2,0,1:T(8,128)} fusion(bf16[16,768,768]{2,1,0:T(8,128)(2,1)} %all-gather.2.cloned.1.call-done, f32[1024,768]{0,1:T(8,128)S(1)} %get-tuple-element.109, f32[768]{0:T(1024)S(1)} %add.145, f32[768]{0:T(1024)S(1)} %mul.298, f32[1024]{0:T(1024)S(1)} %fusion.81, f32[1024]{0:T(1024)S(1)} %broadcast_multiply_fusion.4), kind=kOutput, calls=%fused_computation.31 | convolution fusion | flops 9667608576 | bytes 37763072 | tf_op jit(solution)/shard_map/td,fde->tfe/dot_general | solution.py:132
  280.4 29.9 %multiply_convert_fusion.1 = (bf16[1024,4,768]{2,0,1:T(8,128)(2,1)S(1)}, f32[1024,4,768]{2,0,1:T(8,128)}) fusion(f32[1024,8,768]{2,0,1:T(8,128)} %fusion.9), kind=kLoop, calls=%fused_computation.13 | loop fusion | flops 207618048 | bytes 44040192 | tf_op jit(solution)/shard_map/convert_element_type | solution.py:141
  310.4 9.3 fusion.103
  324.2 24.4 %add_convert_fusion = (bf16[1024,4,768]{2,0,1:T(8,128)(2,1)}, bf16[1024,4,768]{2,0,1:T(8,128)(2,1)}) fusion(f32[1024,4,768]{2,0,1:T(8,128)} %get-tuple-element.84, f32[1024,8,768]{2,0,1:T(8,128)} %fusion.9, bf16[16,768,768]{2,1,0:T(8,128)(2,1)} %all-gather.2.cloned.1.call-done, f32[1024]{0:T(1024)S(1)} %negate_multiply_fusion.2, ...), kind=kOutput, calls=%fused_computation.12 | convolution fusion | flops 4895539200 | bytes 59788288 | tf_op jit(solution)/shard_map/td,fed->tfe/dot_general | solution.py:153
  348.6 24.5 %multiply_reduce_fusion.1 = (f32[768]{0:T(1024)}, f32[1024]{0:T(1024)S(1)}, f32[768]{0:T(1024)}, f32[1024,768]{0,1:T(8,128)}) fusion(f32[1024,768]{0,1:T(8,128)} %copy-done.12, f32[1024]{0:T(1024)S(1)} %fusion.81, f32[1024]{0:T(1024)S(1)} %broadcast_multiply_fusion.4, f32[768]{0:T(1024)S(1)} %mul.298, ...), kind=kOutput, calls=%fused_computation.65 | convolution fusion | flops 9683334144 | bytes 33071104 | tf_op jit(solution)/shard_map/tfe,fde->td/dot_general | solution.py:167
  373.1 3.7 fusion.99
  378.4 3.9 convolution_convert_fusion.1
  387.2 5.2 fusion.57
  392.4 4.6 multiply_reduce_fusion
  405.7 8.2 fusion.77
  413.9 18.5 %fusion.12 = f32[8,768,768]{1,2,0:T(8,128)} fusion(bf16[1024,4,768]{2,0,1:T(8,128)(2,1)} %get-tuple-element.86, bf16[1024,4,768]{2,0,1:T(8,128)(2,1)} %get-tuple-element.85, f32[1024,768]{0,1:T(8,128)} %copy-done.12, f32[768]{0:T(1024)S(1)} %add.145, f32[768]{0:T(1024)S(1)} %mul.298, f32[1024]{0:T(1024)S(1)} %fusion.81, f32[1024]{0:T(1024)S(1)} %broadcast_multiply_fusion.4), kind=kOutput, calls=%fused_computation.34 | convolution fusion | flops 9673900032 | bytes 34617344 | tf_op jit(solution)/shard_map/td,tfe->fde/dot_general | solution.py:164
  432.4 5.2 convolution_bitcast_fusion.2
  440.0 3.7 stack.65
  446.3 3.8 copy.263
  450.0 3.7 stack.64
  456.3 3.8 copy.260
  460.1 3.7 stack.63
  466.6 9.7 convolution_bitcast_fusion
  476.3 25.9 %pad_maximum_fusion = f32[16,768,768]{1,2,0:T(8,128)} fusion(f32[4,768,768]{1,2,0:T(8,128)} %fusion.77, f32[8,768,768]{1,2,0:T(8,128)} %fusion.12, f32[1,768,768]{1,2,0:T(8,128)} %convolution_bitcast_fusion.2, f32[3,768,768]{1,2,0:T(8,128)} %convolution_bitcast_fusion), kind=kLoop, calls=%fused_computation.7 | loop fusion | flops 28311552 | bytes 75497472 | tf_op jit(solution)/shard_map/concatenate | solution.py:202
  502.2 37.9 %copy.279 = f32[16,768,768]{2,0,1:T(8,128)} copy(f32[16,768,768]{1,2,0:T(8,128)} %pad_maximum_fusion) | data formatting | bytes 75497472 | tf_op jit(solution)/shard_map/concatenate | solution.py:202
  540.3 539.0 %reduce-scatter.5.cloned.1.call-done = f32[16,48,768]{2,0,1:T(8,128)} async-done(((f32[16,768,768]{2,0,1:T(8,128)}), f32[16,48,768]{2,0,1:T(8,128)}) %reduce-scatter.5.cloned.1.call-update) | async-done | bytes 2359312 | tf_op jit(solution)/shard_map/reduce_scatter | solution.py:222
  1079.3 4.4 copy.280
  1085.9 3.8 gather_fusion.3
  1089.7 3.8 gather_fusion.5
  1093.5 3.8 gather_fusion.2
  1097.3 7.6 all-reduce.2.cloned.1.call-done
  1104.9 3.8 gather_fusion.4
  1108.7 7.8 select_bitcast_fusion
  1116.5 62.3 %all_to_all.60 = f32[16,1,48,768]{3,2,1,0:T(8,128)} all-to-all(f32[16,1,48,768]{3,2,1,0:T(8,128)} %get-tuple-element.102), channel_id=1, replica_groups=mesh['dp'=2,'zero'=16] {'zero'}, dimensions={0} | all-to-all | bytes 4718592 | tf_op jit(solution)/shard_map/all_to_all | solution.py:226
  1178.8 57.7 %all_to_all.61 = f32[16,1,48,768]{3,2,1,0:T(8,128)} all-to-all(f32[16,1,48,768]{3,2,1,0:T(8,128)S(1)} %get-tuple-element.101), channel_id=1, replica_groups=mesh['dp'=2,'zero'=16] {'zero'}, dimensions={0} | all-to-all | bytes 4718592 | tf_op jit(solution)/shard_map/all_to_all | solution.py:246
  1236.5 57.8 %all_to_all.62 = f32[16,1,48,768]{3,2,1,0:T(8,128)} all-to-all(f32[16,1,48,768]{3,2,1,0:T(8,128)S(1)} %get-tuple-element.105), channel_id=1, replica_groups=mesh['dp'=2,'zero'=16] {'zero'}, dimensions={0} | all-to-all | bytes 4718592 | tf_op jit(solution)/shard_map/all_to_all | solution.py:241
  1294.4 57.8 %all_to_all.63 = f32[16,1,48,768]{3,2,1,0:T(8,128)} all-to-all(f32[16,1,48,768]{3,2,1,0:T(8,128)S(1)} %get-tuple-element.103), channel_id=1, replica_groups=mesh['dp'=2,'zero'=16] {'zero'}, dimensions={0} | all-to-all | bytes 4718592 | tf_op jit(solution)/shard_map/all_to_all | solution.py:235
  1352.1 4.9 all-to-all-start.3
  1364.4 7.7 fusion.37
  1372.1 31.2 %all-to-all-done.3 = f32[16,1,48,768]{3,2,1,0:T(8,128)} async-done(((f32[16,1,48,768]{3,2,1,0:T(8,128)}), f32[16,1,48,768]{3,2,1,0:T(8,128)}, u32[]{:S(2)}, u32[]{:S(2)}) %all-to-all-start.3) | async-done | bytes 2359328 | tf_op jit(solution)/shard_map/all_to_all | solution.py:229
  1403.3 10.2 fusion.31
  1413.5 6.5 fusion.40
  1420.1 7.9 convolution_bitcast_fusion.1
  1428.4 10.4 copy.282
  1438.8 10.9 all-to-all-start.5
  1450.9 10.0 fusion.23
  1463.4 3.6 copy.286
  1467.0 209.3 %reduce-scatter.7.cloned.1.call-done = f32[48,4]{1,0:T(8,128)} async-done(((f32[768,4]{1,0:T(8,128)}), f32[48,4]{1,0:T(8,128)}) %reduce-scatter.7.cloned.1.call-update) | async-done | bytes 784
  1680.2 3.6 copy.283
  1687.2 6.9 gather_fusion.1
  (180 shorter events, 114.0 us)
Async XLA Ops:
  7.2 1076.6 %copy-start = (f32[16,48,768]{2,1,0:T(8,128)S(1)}, f32[16,48,768]{2,1,0:T(8,128)}, u32[]{:S(2)}) copy-start(f32[16,48,768]{2,1,0:T(8,128)} %param.25) | copy-start | bytes 7077892
  7.2 3.1 copy-start.25
  7.2 8.7 copy-start.27
  7.2 8.7 copy-start.24
  7.2 218.0 %all-gather.2.cloned.1.call-start = ((), (), s32[]{:S(2)}) async-start(), calls=%async_computation.8 | async-start | bytes 20054016 | tf_op jit(solution)/shard_map/all_gather | solution.py:101
  10.2 1069.1 %reduce-scatter.5.cloned.1.call-start = ((), (), s32[]{:S(2)}) async-start(), calls=%async_computation.9 | async-start | bytes 40108032 | tf_op jit(solution)/shard_map/reduce_scatter | solution.py:222
  10.3 17.7 %collective-permute-start = (bf16[1,4,48]{2,1,0:T(4,128)(2,1)S(1)}, bf16[1,4,48]{2,1,0:T(4,128)(2,1)S(1)}, u32[]{:S(2)}, u32[]{:S(2)}) collective-permute-start(bf16[1,4,48]{2,1,0:T(4,128)(2,1)S(1)} %get-tuple-element.100), channel_id=1, source_target_pairs={{0,1},{1,0},{2,3},{3,2},{4,5},{5,4},{6,7},{7,6},{8,9},{9,8},{10,11... | collective-permute-start | bytes 1160 | tf_op jit(solution)/shard_map/ppermute | solution.py:33
  27.8 11.6 copy-start.34
  28.0 9.1 copy-start.30
  28.0 4.8 collective-permute-start.1
  32.8 4.1 collective-permute-start.2
  37.0 5.5 collective-permute-start.3
  248.1 2.0 copy-start.2
  250.1 1.6 copy-start.4
  251.7 2.7 copy-start.1
  251.7 2.7 copy-start.8
  257.1 3.4 copy-start.20
  260.5 49.8 %copy-start.12 = (f32[1024,768]{0,1:T(8,128)}, f32[1024,768]{0,1:T(8,128)S(1)}, u32[]{:S(2)}) copy-start(f32[1024,768]{0,1:T(8,128)S(1)} %get-tuple-element.109) | copy-start | bytes 9437188
  310.4 9.4 copy-start.15
  310.4 9.4 copy-start.6
  319.8 4.4 copy-start.10
  376.8 1.6 copy-start.16
  387.2 5.2 copy-start.9
  387.2 9.8 slice-start
  392.4 4.6 slice-start.1
  392.4 12.5 slice-start.2
  397.0 2.3 copy-start.5
  397.0 7.8 slice-start.3
  399.3 3.4 copy-start.3
  402.7 2.1 copy-start.7
  402.7 2.9 copy-start.11
  540.2 564.7 %all-reduce.2.cloned.1.call-start = ((), (), s32[]{:S(2)}) async-start(), calls=%async_computation.10 | async-start | bytes 4718592 | tf_op jit(solution)/shard_map/psum | solution.py:225
  1352.1 51.1 %all-to-all-start.3 = ((f32[16,1,48,768]{3,2,1,0:T(8,128)}), f32[16,1,48,768]{3,2,1,0:T(8,128)}, u32[]{:S(2)}, u32[]{:S(2)}) async-start(f32[16,1,48,768]{3,2,1,0:T(8,128)} %get-tuple-element.104), calls=%async_computation.4 | async-start | bytes 4718592 | tf_op jit(solution)/shard_map/all_to_all | solution.py:229
  1357.0 4.2 copy-start.13
  1361.2 2.5 copy-start.17
  1361.2 3.2 copy-start.19
  1403.2 10.2 copy-start.18
  1438.8 11.0 copy-start.23
  1438.8 11.0 copy-start.22
  1438.8 11.0 copy-start.29
  1438.8 11.1 copy-start.28
  1438.8 12.1 copy-start.31
  1438.8 241.4 %all-to-all-start.5 = ((f32[1,1,3,768,768]{4,1,2,0,3:T(1,128)}), f32[1,1,3,768,768]{4,1,2,0,3:T(1,128)}, u32[]{:S(2)}, u32[]{:S(2)}) async-start(f32[1,1,3,768,768]{4,1,2,0,3:T(1,128)} %copy.282), calls=%async_computation.6 | async-start | bytes 14155776 | tf_op jit(solution)/shard_map/all_to_all | solution.py:253
  1449.7 226.6 %reduce-scatter.7.cloned.1.call-start = ((), (), s32[]{:S(2)}) async-start(), calls=%async_computation.11 | async-start | bytes 417792
  1463.4 216.1 %copy-start.26 = (f32[4,48]{1,0:T(4,128)S(1)}, f32[4,48]{1,0:T(4,128)}, u32[]{:S(2)}) copy-start(f32[4,48]{1,0:T(4,128)} %param.23) | copy-start | bytes 2308
  1463.4 216.1 %copy-start.32 = (f32[4,48]{1,0:T(4,128)S(1)}, f32[4,48]{1,0:T(4,128)}, u32[]{:S(2)}) copy-start(f32[4,48]{1,0:T(4,128)} %param.29) | copy-start | bytes 2308
  1463.4 216.1 %copy-start.33 = (f32[4,48]{1,0:T(4,128)S(1)}, f32[4,48]{1,0:T(4,128)}, u32[]{:S(2)}) copy-start(f32[4,48]{1,0:T(4,128)} %param.28) | copy-start | bytes 2308
  1697.7 2.6 copy-start.14
  (1 other events, 1.4 us)
Sparse Core Ops, SparseCore 0:
  11.3 213.8 all-gather.1
  540.3 538.9 reduce-scatter.4
  1083.9 20.9 all-reduce.1
  1455.4 220.8 reduce-scatter.6
